TPU v7x, 32 devices: a whole 2x2x4 slice. The times are simulated.
32 devices in a mesh: ga: 2 (over x), aa: 8 (over z, y), ba: 2 (over core).
Axes of the slice: x: 2, y: 2, z: 4, core: 2. Of those that a mesh axis runs over, the one named last changes fastest.
Arguments:
- images: bfloat16 [2048, 12, 4096], P(('ga', 'aa', 'ba')), parts along dimension 0, may hold values from -6 to 6
- key_projection: bfloat16 [4096, 512], replicated, may hold values from -0.09375 to 0.09375
- value_projection: bfloat16 [4096, 512], replicated, may hold values from -0.09375 to 0.09375
- key_norm_gain: float32 [128], replicated, may hold values from 0.1 to 1.9
- hidden: bfloat16 [2048, 4096], P(('ga', 'aa'), 'ba'), parts along dimension 0, may hold values from -6 to 6
- shared_query_base: bfloat16 [2048, 2048], P(('ga', 'aa'), 'ba'), parts along dimension 0, may hold values from -220 to 220
- adapter_down_matrix: bfloat16 [8, 4096, 16], P('aa'), may hold values from -0.09375 to 0.09375
- adapter_up_matrix: bfloat16 [8, 16, 2048], P('aa'), may hold values from -1.5 to 1.5
- tenant_adapter_index: int32 [2048, 1], P(('ga', 'aa')), parts along dimension 0, may hold values from 0 to 7; in each aligned block of 128 rows (0 to 127, 128 to 255, ...) at most 32 rows name the same one
- used_tile_count: int32 [2048], P(('ga', 'aa', 'ba')), parts along dimension 0, may hold values from 1 to 4
Outputs:
- attended: bfloat16 [2048, 2048], P(('ga', 'aa', 'ba')), parts along dimension 0
There are 2 independent parts, one for each index of `ga`. A program takes and returns all parts, laid end to end along the dimension named above; an argument that names none is the same for every part. Nothing has to cross between parts.
Inputs may be any that keep to these rules, and one draw needn't show every extreme that they name: `tenant_adapter_index`: among the 128 requests of one index of aa (aligned blocks) no adapter is named more than 32 times.
All inputs are finite; a program needn't handle non-finite values.
Results may differ from a plain program's by a relative error of at most 0.012.
The roundings to bfloat16 on the way count: a program that leaves them out, or rounds other values in their place, can miss the bound.
Values may be sent and summed in bfloat16 or wider, within the bound.
A program may use at most 128 MiB of HBM per device.

v0:
```python
import math

import jax
import jax.numpy as jnp
from jax import lax
from jax.sharding import PartitionSpec as P

TILE_TOKENS = 3


def on_device(
    images,
    key_projection,
    value_projection,
    key_norm_gain,
    hidden,
    shared_query_base,
    adapter_down_matrix,
    adapter_up_matrix,
    tenant_adapter_index,
    used_tile_count,
):
    requests = hidden.shape[0]
    half_model = hidden.shape[1]
    half_query = shared_query_base.shape[1]
    head_size = key_norm_gain.shape[0]
    heads_kv = key_projection.shape[1] // head_size
    bank_count = lax.axis_size("aa")
    slots_most = 2 * requests // bank_count
    our_side = lax.axis_index("ba")
    owner_ids = tenant_adapter_index[:, 0]
    owner_hot = (owner_ids[:, None] == jnp.arange(bank_count, dtype=jnp.int32)[None, :]).astype(
        jnp.float32
    )
    lower_ones = (jnp.arange(requests)[:, None] > jnp.arange(requests)[None, :]).astype(
        jnp.bfloat16
    )
    before = jnp.dot(lower_ones, owner_hot.astype(jnp.bfloat16), preferred_element_type=jnp.float32)
    rank_in = jnp.sum(before * owner_hot, axis=1)
    slot_hot = (rank_in[:, None] == jnp.arange(slots_most, dtype=jnp.float32)[None, :]).astype(
        jnp.float32
    )
    placing = (
        (owner_hot[:, :, None] * slot_hot[:, None, :])
        .reshape(requests, bank_count * slots_most)
        .astype(jnp.bfloat16)
    )
    down_half = lax.dynamic_slice_in_dim(
        adapter_down_matrix[0], our_side * half_model, half_model, 0
    )
    up_half = lax.dynamic_slice_in_dim(adapter_up_matrix[0], our_side * half_query, half_query, 1)
    packed = lax.dot_general(
        placing, hidden, (((0,), (0,)), ((), ())), preferred_element_type=jnp.float32
    )
    received_rows = lax.all_to_all(
        packed.astype(jnp.bfloat16).reshape(bank_count, slots_most, hidden.shape[1]),
        "aa",
        split_axis=0,
        concat_axis=0,
        tiled=True,
    )
    low_part = jnp.dot(
        received_rows.reshape(-1, half_model), down_half, preferred_element_type=jnp.float32
    )
    reduced_rank_part = lax.psum(low_part, "ba")
    raised_output = jnp.dot(
        reduced_rank_part.astype(jnp.bfloat16), up_half, preferred_element_type=jnp.float32
    )
    raised_output = raised_output.astype(jnp.bfloat16).reshape(
        received_rows.shape[0], received_rows.shape[1], half_query
    )
    returned = lax.all_to_all(raised_output, "aa", split_axis=0, concat_axis=0, tiled=True)
    flat_back = returned.reshape(bank_count * slots_most, returned.shape[2])
    delta_half = jnp.dot(placing, flat_back, preferred_element_type=jnp.float32)
    query_half = (shared_query_base.astype(jnp.float32) + delta_half).astype(jnp.bfloat16)
    query_rows = lax.all_to_all(query_half, "ba", split_axis=0, concat_axis=1, tiled=True)
    requests_here = images.shape[0]
    local_rows = images.shape[1]
    flattened_rows = images.reshape(requests_here * local_rows, images.shape[2])
    unnormed_keys = jnp.dot(
        flattened_rows, key_projection, preferred_element_type=jnp.float32
    ).reshape(requests_here, local_rows, heads_kv, head_size)
    key_scale = lax.rsqrt(jnp.mean(unnormed_keys * unnormed_keys, axis=-1, keepdims=True) + 1e-06)
    keys_local = (unnormed_keys * key_scale * key_norm_gain).astype(jnp.bfloat16)
    values_local = jnp.dot(
        flattened_rows, value_projection, preferred_element_type=jnp.float32
    ).astype(jnp.bfloat16)
    values_local = values_local.reshape(requests_here, local_rows, heads_kv, head_size)
    query_group_width = query_rows.shape[1] // (heads_kv * head_size)
    query_four_axes = query_rows.reshape(requests_here, heads_kv, query_group_width, head_size)
    scores = jnp.einsum(
        "rkgd,rjkd->rkgj", query_four_axes, keys_local, preferred_element_type=jnp.float32
    ) / math.sqrt(head_size)
    position = jnp.arange(local_rows, dtype=jnp.int32) // TILE_TOKENS
    valid_rows = position[None, :] < used_tile_count[:, None]
    key_mask = valid_rows[:, None, None, :]
    masked = jnp.where(key_mask, scores, -1e30)
    score_peak = jnp.max(masked, axis=-1)
    weights = jnp.where(key_mask, jnp.exp(masked - score_peak[..., None]), 0.0)
    weight_total = jnp.sum(weights, axis=-1)
    weighted = jnp.einsum(
        "rkgj,rjkd->rkgd",
        weights.astype(jnp.bfloat16),
        values_local,
        preferred_element_type=jnp.float32,
    )
    attended = (weighted / weight_total[..., None]).reshape(requests_here, -1).astype(jnp.bfloat16)
    return attended


def solution(mesh):
    placed = (
        P(("ga", "aa", "ba"), None, None),
        P(),
        P(),
        P(),
        P(("ga", "aa"), "ba"),
        P(("ga", "aa"), "ba"),
        P("aa", None, None),
        P("aa", None, None),
        P(("ga", "aa"), None),
        P(("ga", "aa", "ba")),
    )
    return jax.shard_map(
        on_device,
        mesh=mesh,
        in_specs=placed,
        out_specs=P(("ga", "aa", "ba"), None),
        check_vma=False,
    )
```

profile of v0, /device:TPU:1, one launch (start us, length us, event | category | flops | bytes accessed | tf_op | source)
XLA Modules:
  0.0 77.3 jit_solution(13256028796307270376)
XLA Ops:
  0.0 0.9 %fusion.10 = f32[128]{0:T(128)S(1)} fusion(s32[128]{0:T(128)} %bitcast.46), kind=kOutput, calls=%fused_computation.19 | convolution fusion | flops 284544 | bytes 1024 | tf_op jit(solution)/shard_map/dot_general | solution.py:38
  0.9 0.7 fusion.21
  1.6 1.4 %convolution_convert_fusion = bf16[256,2048]{1,0:T(8,128)(2,1)} fusion(bf16[128,256]{0,1:T(8,128)(2,1)S(1)} %bitcast.45, bf16[128,2048]{1,0:T(8,128)(2,1)S(1)} %copy-done), kind=kOutput, calls=%fused_computation.3 | convolution fusion | flops 134742016 | bytes 1638400 | tf_op jit(solution)/shard_map/dot_general | solution.py:52
  3.0 6.4 %all-to-all-start = ((bf16[8,32,2048]{2,1,0:T(8,128)(2,1)}), bf16[8,32,2048]{2,1,0:T(8,128)(2,1)S(1)}, u32[]{:S(2)}, u32[]{:S(2)}) async-start(bf16[8,32,2048]{2,1,0:T(8,128)(2,1)} %bitcast.2), calls=%async_computation | async-start | bytes 2097152 | tf_op jit(solution)/shard_map/all_to_all | solution.py:55
  9.4 9.6 %copy.18 = bf16[64,12,4096]{2,1,0:T(8,128)(2,1)} copy(bf16[64,12,4096]{2,0,1:T(8,128)(2,1)} %param.10) | data formatting | bytes 12582912 | tf_op args[0]
  19.0 9.9 %reshape.129 = bf16[768,4096]{1,0:T(8,128)(2,1)} reshape(bf16[64,12,4096]{2,1,0:T(8,128)(2,1)} %copy.18) | data formatting | bytes 12582912 | tf_op jit(solution)/shard_map/reshape | solution.py:79
  28.8 6.4 %copy.21 = bf16[512,4096]{1,0:T(8,128)(2,1)} copy(bf16[512,4096]{0,1:T(8,128)(2,1)} %bitcast.40) | data formatting | bytes 8388608 | tf_op jit(solution)/shard_map/dot_general | solution.py:80
  35.3 6.7 %multiply_reduce_fusion = (f32[64,12,4]{0,2,1:T(4,128)S(1)}, f32[64,12,4,128]{3,0,2,1:T(8,128)S(1)}) fusion(bf16[4,128,4096,1]{2,1,0,3:T(8,128)(2,1)} %bitcast.41, bf16[64,12,4096]{2,0,1:T(8,128)(2,1)} %param.10), kind=kOutput, calls=%fused_computation.5 | convolution fusion | flops 3222008832 | bytes 12070912 | tf_op jit(solution)/shard_map/dot_general | solution.py:80
  42.0 0.4 fusion.14
  42.4 4.6 %psum.7 = bf16[256,16]{1,0:T(8,128)(2,1)S(1)} all-reduce(f32[256,16]{1,0:T(8,128)S(1)} %fusion.14), channel_id=1, replica_groups=mesh['ga'=2,'aa'=8,'ba'=2] {'ba'}, use_global_device_ids=true, to_apply=%region_1.0 | all-reduce | flops 4096 | bytes 24576 | tf_op jit(solution)/shard_map/psum | solution.py:65
  47.1 1.1 %convolution_convert_fusion.2 = bf16[256,1024]{1,0:T(8,128)(2,1)} fusion(bf16[256,16]{1,0:T(8,128)(2,1)S(1)} %psum.7, bf16[1,16,2048]{2,1,0:T(8,128)(2,1)S(1)} %copy-done.4, s32[]{:T(128)S(6)} %select_n.24), kind=kOutput, calls=%fused_computation.8 | convolution fusion | flops 8650752 | bytes 622596 | tf_op jit(solution)/shard_map/dot_general | solution.py:66
  48.2 5.7 %all-to-all-start.1 = ((bf16[8,32,1024]{2,1,0:T(8,128)(2,1)}), bf16[8,32,1024]{2,1,0:T(8,128)(2,1)S(1)}, u32[]{:S(2)}, u32[]{:S(2)}) async-start(bf16[8,32,1024]{2,1,0:T(8,128)(2,1)} %bitcast.6), calls=%async_computation.1 | async-start | bytes 1048576 | tf_op jit(solution)/shard_map/all_to_all | solution.py:72
  53.9 8.3 %convolution_convert_fusion.1 = bf16[768,512]{1,0:T(8,128)(2,1)} fusion(bf16[768,4096]{1,0:T(8,128)(2,1)} %reshape.129, bf16[4096,512]{1,0:T(8,128)(2,1)} %param.12), kind=kOutput, calls=%fused_computation.6 | convolution fusion | flops 3221618688 | bytes 11272192 | tf_op jit(solution)/shard_map/dot_general | solution.py:85
  62.3 2.5 %reshape.130 = bf16[64,12,4,128]{3,2,1,0:T(4,128)(2,1)} reshape(bf16[768,512]{1,0:T(8,128)(2,1)} %convolution_convert_fusion.1) | data formatting | bytes 1572864 | tf_op jit(solution)/shard_map/reshape | solution.py:88
  64.8 0.1 broadcast_compare_fusion
  64.9 1.4 %multiply_convert_fusion = bf16[64,12,4,128]{3,0,2,1:T(8,128)(2,1)} fusion(f32[64,12,4,128]{3,0,2,1:T(8,128)S(1)} %get-tuple-element.6, f32[128]{0:T(128)S(1)} %copy-done.6, f32[64,12,4]{0,2,1:T(4,128)S(1)} %add_rsqrt_fusion), kind=kLoop, calls=%fused_computation.4 | loop fusion | flops 1179648 | bytes 2372096 | tf_op jit(solution)/shard_map/convert_element_type | solution.py:84
  66.2 1.5 %all-to-all-done.1 = bf16[8,32,1024]{2,1,0:T(8,128)(2,1)S(1)} async-done(((bf16[8,32,1024]{2,1,0:T(8,128)(2,1)}), bf16[8,32,1024]{2,1,0:T(8,128)(2,1)S(1)}, u32[]{:S(2)}, u32[]{:S(2)}) %all-to-all-start.1) | async-done | bytes 524320 | tf_op jit(solution)/shard_map/all_to_all | solution.py:72
  67.8 0.3 fusion.9
  68.0 5.2 %all_to_all.26 = bf16[2,64,1024]{2,1,0:T(8,128)(2,1)S(1)} all-to-all(bf16[2,64,1024]{2,1,0:T(8,128)(2,1)S(1)} %bitcast.44), channel_id=1, replica_groups=mesh['ga'=2,'aa'=8,'ba'=2] {'ba'}, dimensions={0} | all-to-all | bytes 524288 | tf_op jit(solution)/shard_map/all_to_all | solution.py:76
  73.2 0.3 copy.15
  73.5 0.2 reshape.128
  73.6 2.3 %fusion.26 = (f32[64,4,4]{2,1,0:T(4,128)S(1)}, bf16[64,4,4,12]{3,2,1,0:T(4,128)(2,1)S(1)}) fusion(pred[64,12]{1,0:T(8,128)(4,1)S(1)} %broadcast_compare_fusion, bf16[64,4,4,128]{3,2,1,0:T(4,128)(2,1)S(1)} %reshape.128, bf16[64,12,4,128]{3,0,2,1:T(8,128)(2,1)} %multiply_convert_fusion), kind=kOutput, calls=%fused_computation.44 | convolution fusion | flops 3219467 | bytes 1078016 | tf_op jit(solution)/shard_map/sub | solution.py:99
  76.0 0.5 fusion.8
  76.5 0.9 %convert_element_type.69 = bf16[64,2048]{1,0:T(8,128)(2,1)} reshape(bf16[64,4,4,128]{3,2,1,0:T(4,128)(2,1)S(1)} %fusion.8) | data formatting | bytes 524288 | tf_op jit(solution)/shard_map/convert_element_type | solution.py:107
  (19 shorter events, 0.1 us)
Async XLA Ops:
  0.0 1.6 %copy-start = (bf16[128,2048]{1,0:T(8,128)(2,1)S(1)}, bf16[128,2048]{1,0:T(8,128)(2,1)}, u32[]{:S(2)}) copy-start(bf16[128,2048]{1,0:T(8,128)(2,1)} %param.14) | copy-start | bytes 1572868
  3.0 39.0 %all-to-all-start = ((bf16[8,32,2048]{2,1,0:T(8,128)(2,1)}), bf16[8,32,2048]{2,1,0:T(8,128)(2,1)S(1)}, u32[]{:S(2)}, u32[]{:S(2)}) async-start(bf16[8,32,2048]{2,1,0:T(8,128)(2,1)} %bitcast.2), calls=%async_computation | async-start | bytes 2097152 | tf_op jit(solution)/shard_map/all_to_all | solution.py:55
  35.2 6.8 %copy-start.3 = (bf16[1,4096,16]{1,2,0:T(8,128)(2,1)S(1)}, bf16[1,4096,16]{1,2,0:T(8,128)(2,1)}, u32[]{:S(2)}) copy-start(bf16[1,4096,16]{1,2,0:T(8,128)(2,1)} %param.16) | copy-start | bytes 393220
  35.3 11.8 %copy-start.4 = (bf16[1,16,2048]{2,1,0:T(8,128)(2,1)S(1)}, bf16[1,16,2048]{2,1,0:T(8,128)(2,1)}, u32[]{:S(2)}) copy-start(bf16[1,16,2048]{2,1,0:T(8,128)(2,1)} %param.17) | copy-start | bytes 196612
  48.2 19.6 %all-to-all-start.1 = ((bf16[8,32,1024]{2,1,0:T(8,128)(2,1)}), bf16[8,32,1024]{2,1,0:T(8,128)(2,1)S(1)}, u32[]{:S(2)}, u32[]{:S(2)}) async-start(bf16[8,32,1024]{2,1,0:T(8,128)(2,1)} %bitcast.6), calls=%async_computation.1 | async-start | bytes 1048576 | tf_op jit(solution)/shard_map/all_to_all | solution.py:72
  53.9 10.8 %copy-start.5 = (s32[64]{0:T(128)S(1)}, s32[64]{0:T(128)}, u32[]{:S(2)}) copy-start(s32[64]{0:T(128)} %param.19) | copy-start | bytes 772
  53.9 10.9 %copy-start.6 = (f32[128]{0:T(128)S(1)}, f32[128]{0:T(128)}, u32[]{:S(2)}) copy-start(f32[128]{0:T(128)} %param.13) | copy-start | bytes 1540
  62.3 5.5 %copy-start.2 = (bf16[128,1024]{1,0:T(8,128)(2,1)S(1)}, bf16[128,1024]{1,0:T(8,128)(2,1)}, u32[]{:S(2)}) copy-start(bf16[128,1024]{1,0:T(8,128)(2,1)} %param.15) | copy-start | bytes 786436
  66.2 9.7 %copy-start.1 = (bf16[64,12,4,128]{3,2,1,0:T(4,128)(2,1)S(1)}, bf16[64,12,4,128]{3,2,1,0:T(4,128)(2,1)}, u32[]{:S(2)}) copy-start(bf16[64,12,4,128]{3,2,1,0:T(4,128)(2,1)} %reshape.130) | copy-start | bytes 2359300
where the time goes:
time: 78.5 us; the launch traced here: 77.3 us
  local copies, waits for them, and re-layouts  29.7 us (38%)
  matrix products  21.9 us (28%)
  starting transfers between devices  12.1 us (15%)
  blocking collectives  9.82 us (13%)
  other arithmetic  2.18 us (3%)
  waiting for transfers between devices  1.51 us (2%)
    reshape x1, local copies, waits for them, and re-layouts, on_device(): flattened_rows = images.reshape(requests_here * local_rows, images.shape[2])  9.85 us
    unnamed x15, local copies, waits for them, and re-layouts  9.64 us
    dot_general x1, matrix products, on_device(): jnp.dot(flattened_rows, value_projection, preferred_element_type=jnp.floa...  8.33 us
    dot_general x1, matrix products, on_device(): jnp.dot(flattened_rows, key_projection, preferred_element_type=jnp.float32)  6.74 us
    dot_general x1, local copies, waits for them, and re-layouts, on_device(): jnp.dot(flattened_rows, key_projection, preferred_element_type=jnp.float32)  6.41 us
    all_to_all x1, starting transfers between devices, on_device(): lax.all_to_all(packed.astype(jnp.bfloat16).reshape(bank_count, slots_most...  6.37 us
    all_to_all x1, starting transfers between devices, on_device(): lax.all_to_all(raised_output, 'aa', split_axis=0, concat_axis=0, tiled=True)  5.72 us
    all_to_all x1, blocking collectives, on_device(): lax.all_to_all(query_half, 'ba', split_axis=0, concat_axis=1, tiled=True)  5.18 us
  transfers between devices with their start and end apart: 2, of which 1 were waited for; matrix products, arithmetic and copies ran while one was open for 58% of the time, Pallas kernels for 0%

commit v1 on v0

v1 whole, which is shorter than its diff:
```python
import functools
import math

import jax
import jax.numpy as jnp
from jax import lax
from jax.experimental import pallas as pl
from jax.experimental.pallas import tpu as pltpu
from jax.sharding import PartitionSpec as P

TILE_TOKENS = 3
REQUEST_BLOCK = 16
CHUNKS = 8
MESH = pl.DeviceIdType.MESH
NT = (((1,), (1,)), ((), ()))


def grid_of(count):
    inner = max(d for d in range(1, count + 1) if count % d == 0 and d * d <= count)
    return count // inner, inner


def kernel(
    outer, inner, images, wk_hbm, wv_hbm, hidden, base, down, up, gain, ids, used, out,
    img, wk, wv, acc, keys, vals, all_down, all_up, hid, bas,
    in_sem, own_sem, zs, zr, ys, yr, ps, pr, xs, xr,
):
    chunks, rows, depth = img.shape
    _, here, half_model = hid.shape
    half_query = bas.shape[2]
    rank = down.shape[0]
    head = gain.shape[1]
    width = wk.shape[2]
    heads_kv = width // head
    group = 2 * half_query // width
    tokens = rows // here

    me = lax.axis_index("aa")
    side = lax.axis_index("ba")
    other = 1 - side
    z, y = me // inner, lax.rem(me, inner)

    def at_z(d):
        return {"aa": lax.rem(z + d, outer) * inner + y}

    def at_y(e):
        return {"aa": z * inner + lax.rem(y + e, inner)}

    partner = {"ba": other}

    loads = []
    for c in range(chunks):
        cols = pl.ds(c * depth, depth)
        loads.append([
            pltpu.make_async_copy(images.at[:, cols], img.at[c], in_sem.at[c, 0]),
            pltpu.make_async_copy(wk_hbm.at[cols], wk.at[c], in_sem.at[c, 1]),
            pltpu.make_async_copy(wv_hbm.at[cols], wv.at[c], in_sem.at[c, 2]),
        ])
    for copy in loads[0]:
        copy.start()

    def halves(ref, s, size):
        return ref.at[:, pl.ds(pl.multiple_of(s * size, 128), size)]

    mine = pl.ds(pl.multiple_of(side * here, here), here)
    theirs = pl.ds(pl.multiple_of(other * here, here), here)

    barrier = pltpu.get_barrier_semaphore()
    greeted = [at_z(d) for d in range(1, outer)] + [at_y(e) for e in range(1, inner)] + [partner]
    for device in greeted:
        pl.semaphore_signal(barrier, inc=1, device_id=device, device_id_type=MESH)
    for copies in loads[1:]:
        for copy in copies:
            copy.start()
    local = [
        pltpu.make_async_copy(hidden.at[mine], hid.at[side], own_sem.at[0]),
        pltpu.make_async_copy(base.at[mine], bas.at[side], own_sem.at[1]),
    ]
    own_rows = pl.ds(pl.multiple_of(me * rank, rank), rank)
    for s in range(2):
        local.append(pltpu.make_async_copy(
            halves(down, s, half_model), all_down.at[s, own_rows], own_sem.at[2 + s]))
        local.append(pltpu.make_async_copy(
            halves(up, s, half_query), all_up.at[s, own_rows], own_sem.at[4 + s]))
    pl.semaphore_wait(barrier, len(greeted))

    def block_rows(d, e):
        b = lax.rem(z + (outer - d), outer) * inner + lax.rem(y + (inner - e), inner)
        return pl.ds(pl.multiple_of(b * rank, rank), rank)

    def send(d, e, device, ssem, rsem, slot):
        r = block_rows(d, e)
        if d == 0 and e == 0:
            sources = (halves(down, side, half_model), halves(up, side, half_query))
        else:
            sources = (all_down.at[side, r], all_up.at[side, r])
        targets = (all_down.at[side, r], all_up.at[side, r])
        made = []
        for i in range(2):
            made.append(pltpu.make_async_remote_copy(
                src_ref=sources[i], dst_ref=targets[i],
                send_sem=ssem.at[slot, i], recv_sem=rsem.at[slot, i],
                device_id=device, device_id_type=MESH))
        for copy in made:
            copy.start()
        return made

    near = sorted(range(1, outer), key=lambda d: min(d, outer - d))
    z_copies = {d: send(0, 0, at_z(d), zs, zr, d) for d in near}
    y_copies = {(0, e): send(0, 0, at_y(e), ys, yr, e) for e in range(1, inner)}
    swaps = []
    for i, (src, dst) in enumerate(((hidden, hid), (base, bas))):
        swaps.append(pltpu.make_async_remote_copy(
            src_ref=src.at[theirs], dst_ref=dst.at[side],
            send_sem=xs.at[i], recv_sem=xr.at[i], device_id=partner, device_id_type=MESH))
    for copy in swaps:
        copy.start()
    for copy in local:
        copy.start()
    p_copies = []

    def arrived(copies):
        for copy in copies:
            copy.wait_recv()

    def pass_z(d):
        arrived(z_copies[d])
        for e in range(1, inner):
            y_copies[d, e] = send(d, 0, at_y(e), ys, yr, d * inner + e)
        p_copies.extend(send(d, 0, partner, ps, pr, d * inner))

    def pass_y(d):
        for e in range(1, inner):
            arrived(y_copies[d, e])
            p_copies.extend(send(d, e, partner, ps, pr, d * inner + e))

    jobs = [functools.partial(pass_z, d) for d in near] + [
        functools.partial(pass_y, d) for d in [0] + near]
    first = chunks // 2
    for c in range(chunks):
        for copy in loads[c]:
            copy.wait()
        for part, w in enumerate((wk, wv)):
            cols = slice(part * width, (part + 1) * width)
            term = jnp.dot(img[c], w[c], preferred_element_type=jnp.float32)
            if c == 0:
                acc[:, cols] = term
            else:
                acc[:, cols] += term
        if c >= first and len(jobs) > outer:
            jobs.pop(0)()
    while len(jobs) > outer:
        jobs.pop(0)()

    g = gain[...]
    for k in range(heads_kv):
        cols = slice(k * head, (k + 1) * head)
        x = acc[:, cols]
        scale = lax.rsqrt(jnp.mean(x * x, axis=-1, keepdims=True) + 1e-06)
        keys[:, :, cols] = (x * scale * g).astype(jnp.bfloat16).reshape(tokens, here, head)
    vals[...] = acc[:, width:].astype(jnp.bfloat16).reshape(tokens, here, width)

    for job in jobs:
        job()
    for copy in local:
        copy.wait()
    arrived(swaps)
    arrived(p_copies)

    id_row = ids[...]
    requests = id_row.shape[1]
    row_at = lax.broadcasted_iota(jnp.int32, (here, requests), 0) + side * here
    col_at = lax.broadcasted_iota(jnp.int32, (here, requests), 1)
    id_col = jnp.sum(jnp.where(row_at == col_at, id_row, 0), axis=1, keepdims=True)
    low = lax.dot_general(hid[0], all_down[0], NT, preferred_element_type=jnp.float32)
    low += lax.dot_general(hid[1], all_down[1], NT, preferred_element_type=jnp.float32)
    lane = lax.broadcasted_iota(jnp.int32, low.shape, 1)
    owned = (lane >= id_col * rank) & (lane < id_col * rank + rank)
    low = jnp.where(owned, low, 0.0).astype(jnp.bfloat16)
    queries = []
    for s in range(2):
        delta = jnp.dot(low, all_up[s], preferred_element_type=jnp.float32).astype(jnp.bfloat16)
        queries.append(
            (bas[s].astype(jnp.float32) + delta.astype(jnp.float32)).astype(jnp.bfloat16))
    queries = jnp.concatenate(queries, axis=1)

    eye = lax.broadcasted_iota(jnp.int32, (here, here), 0) == lax.broadcasted_iota(
        jnp.int32, (here, here), 1)
    used_col = jnp.sum(jnp.where(eye, used[...], 0), axis=1, keepdims=True)
    nb = REQUEST_BLOCK
    shape = (group * nb, tokens * nb)
    r_at = lax.broadcasted_iota(jnp.int32, shape, 0)
    c_at = lax.broadcasted_iota(jnp.int32, shape, 1)
    same = (r_at & (nb - 1)) == (c_at & (nb - 1))
    for b in range(here // nb):
        rs = slice(b * nb, (b + 1) * nb)
        limit = jnp.concatenate([used_col[rs]] * group, axis=0) * (TILE_TOKENS * nb)
        mask = same & (c_at < limit)
        for k in range(heads_kv):
            cols = slice(k * head, (k + 1) * head)
            kb = keys[:, rs, cols].reshape(tokens * nb, head)
            vb = vals[:, rs, cols].reshape(tokens * nb, head)
            q = jnp.concatenate(
                [queries[rs, (k * group + i) * head:(k * group + i + 1) * head]
                 for i in range(group)], axis=0)
            scores = lax.dot_general(q, kb, NT, preferred_element_type=jnp.float32)
            scores = jnp.where(mask, scores * (1.0 / math.sqrt(head)), -1e30)
            peak = jnp.max(scores, axis=1, keepdims=True)
            weights = jnp.where(mask, jnp.exp(scores - peak), 0.0)
            total = jnp.sum(weights, axis=1, keepdims=True)
            mixed = jnp.dot(weights.astype(jnp.bfloat16), vb, preferred_element_type=jnp.float32)
            mixed = (mixed / total).astype(jnp.bfloat16)
            for i in range(group):
                out[rs, (k * group + i) * head:(k * group + i + 1) * head] = (
                    mixed[i * nb:(i + 1) * nb])

    for copies in list(z_copies.values()) + list(y_copies.values()) + [p_copies, swaps]:
        for copy in copies:
            copy.wait_send()


def on_device(
    images,
    key_projection,
    value_projection,
    key_norm_gain,
    hidden,
    shared_query_base,
    adapter_down_matrix,
    adapter_up_matrix,
    tenant_adapter_index,
    used_tile_count,
):
    here, tokens, model = images.shape
    rows = here * tokens
    width = key_projection.shape[1]
    half_model = hidden.shape[1]
    half_query = shared_query_base.shape[1]
    rank = adapter_down_matrix.shape[2]
    count = lax.axis_size("aa")
    outer, inner = grid_of(count)
    flat = jnp.transpose(images, (1, 0, 2)).reshape(rows, model)
    down = jnp.transpose(adapter_down_matrix[0])
    depth = model // CHUNKS
    bf16 = jnp.bfloat16
    hbm = pl.BlockSpec(memory_space=pl.ANY)
    vmem = pl.BlockSpec(memory_space=pltpu.VMEM)
    dma = pltpu.SemaphoreType.DMA
    return pl.pallas_call(
        functools.partial(kernel, outer, inner),
        out_shape=jax.ShapeDtypeStruct((here, 2 * half_query), bf16),
        in_specs=[hbm] * 7 + [vmem] * 3,
        out_specs=vmem,
        scratch_shapes=[
            pltpu.VMEM((CHUNKS, rows, depth), bf16),
            pltpu.VMEM((CHUNKS, depth, width), bf16),
            pltpu.VMEM((CHUNKS, depth, width), bf16),
            pltpu.VMEM((rows, 2 * width), jnp.float32),
            pltpu.VMEM((tokens, here, width), bf16),
            pltpu.VMEM((tokens, here, width), bf16),
            pltpu.VMEM((2, count * rank, half_model), bf16),
            pltpu.VMEM((2, count * rank, half_query), bf16),
            pltpu.VMEM((2, here, half_model), bf16),
            pltpu.VMEM((2, here, half_query), bf16),
            dma((CHUNKS, 3)),
            dma((6,)),
            dma((outer, 2)),
            dma((outer, 2)),
            dma((count, 2)),
            dma((count, 2)),
            dma((count, 2)),
            dma((count, 2)),
            dma((2,)),
            dma((2,)),
        ],
        compiler_params=pltpu.CompilerParams(
            collective_id=0, has_side_effects=True, vmem_limit_bytes=60 * 1024 * 1024
        ),
    )(
        flat,
        key_projection,
        value_projection,
        hidden,
        shared_query_base,
        down,
        adapter_up_matrix[0],
        key_norm_gain[None, :],
        tenant_adapter_index.reshape(1, -1),
        used_tile_count[None, :],
    )


def solution(mesh):
    placed = (
        P(("ga", "aa", "ba"), None, None),
        P(),
        P(),
        P(),
        P(("ga", "aa"), "ba"),
        P(("ga", "aa"), "ba"),
        P("aa", None, None),
        P("aa", None, None),
        P(("ga", "aa"), None),
        P(("ga", "aa", "ba")),
    )
    return jax.shard_map(
        on_device,
        mesh=mesh,
        in_specs=placed,
        out_specs=P(("ga", "aa", "ba"), None),
        check_vma=False,
    )
```

time: 78.5 us -> 29 us (0.37); the launches traced: 77.3 us -> 28.8 us
  local copies, waits for them, and re-layouts: 29.7 us -> 1.67 us
  Pallas kernels: 0 us -> 27.1 us
  matrix products: 21.9 us -> 0 us
  starting transfers between devices: 12.1 us -> 0 us
  blocking collectives: 9.82 us -> 0 us
  other arithmetic: 2.18 us -> 0 us
  waiting for transfers between devices: 1.51 us -> 0 us
    pallas_call x0 -> x1, Pallas kernels: none -> 27.1 us  [on_device(): pl.pallas_call(functools.partial(kernel, outer, inner), out_shape=jax.Sha...]
    dot_general x8 -> x0, matrix products: 19.6 us -> none  [the longest x1 8.33 us: on_device(): jnp.dot(flattened_rows, value_projection, preferred_element_type=jnp.floa...]
    reshape x3 -> x0, local copies, waits for them, and re-layouts: 12.5 us -> none  [the longest x1 9.85 us: on_device(): flattened_rows = images.reshape(requests_here * local_rows, images.shape[2])]
    all_to_all x2 -> x0, starting transfers between devices: 12.1 us -> none  [the longest x1 6.37 us: on_device(): lax.all_to_all(packed.astype(jnp.bfloat16).reshape(bank_count, slots_most...]
    unnamed x15 -> x1, local copies, waits for them, and re-layouts: 9.64 us -> 1.67 us
    dot_general x1 -> x0, local copies, waits for them, and re-layouts: 6.41 us -> none  [on_device(): jnp.dot(flattened_rows, key_projection, preferred_element_type=jnp.float32)]
    all_to_all x1 -> x0, blocking collectives: 5.18 us -> none  [on_device(): lax.all_to_all(query_half, 'ba', split_axis=0, concat_axis=1, tiled=True)]
    psum x1 -> x0, blocking collectives: 4.64 us -> none  [on_device(): reduced_rank_part = lax.psum(low_part, 'ba')]
  transfers between devices with their start and end apart: 2 -> 0, of which waited for: 1 -> 0; matrix products, arithmetic and copies ran while one was open for 58% -> 0% of each run, Pallas kernels for 0% -> 0%
where the time goes in v1:
time: 29 us; the launch traced here: 28.8 us
  Pallas kernels  27.1 us (93%)
  local copies, waits for them, and re-layouts  1.67 us (6%)
    pallas_call x1, Pallas kernels, on_device(): pl.pallas_call(functools.partial(kernel, outer, inner), out_shape=jax.Sha...  27.1 us
    unnamed x1, local copies, waits for them, and re-layouts  1.67 us

profile of v1, /device:TPU:1, one launch (start us, length us, event | category | flops | bytes accessed | tf_op | source)
XLA Modules:
  0.0 28.8 jit_solution(17181318834770552848)
XLA Ops:
  0.0 27.1 %shard_map.100 = bf16[64,2048]{1,0:T(8,128)(2,1)} custom-call(bf16[768,4096]{1,0:T(8,128)(2,1)} %bitcast.10, bf16[4096,512]{1,0:T(8,128)(2,1)} %wk_hbm.1, bf16[4096,512]{1,0:T(8,128)(2,1)} %wv_hbm.1, bf16[128,2048]{1,0:T(8,128)(2,1)} %hidden.1, bf16[128,1024]{1,0:T(8,128)(2,1)} %base.1, bf16[16,4096]{1,0:T(8,128)(2,1)} %bitcast.11, ...), custom_call_target="tpu_custom_call" | custom-call | tf_op jit(solution)/shard_map/pallas_call | solution.py:249
  27.1 1.7 %copy.12 = bf16[64,2048]{1,0:T(8,128)(2,1)} copy(bf16[64,2048]{1,0:T(8,128)(2,1)} %shard_map.100) | data formatting | bytes 524288

commit v2 on v1

v2 whole, which is shorter than its diff:
```python
import functools
import math

import jax
import jax.numpy as jnp
from jax import lax
from jax.experimental import pallas as pl
from jax.experimental.pallas import tpu as pltpu
from jax.sharding import PartitionSpec as P

TILE_TOKENS = 3
REQUEST_BLOCK = 16
CHUNKS = 8
MESH = pl.DeviceIdType.MESH
NT = (((1,), (1,)), ((), ()))


def grid_of(count):
    inner = max(d for d in range(1, count + 1) if count % d == 0 and d * d <= count)
    return count // inner, inner


def kernel(
    outer, inner, images, wk_hbm, wv_hbm, hidden, base, down, up, gain, ids, used, out,
    img, wk, wv, acc, keys, vals, all_down, all_up, hid, bas,
    in_sem, own_sem, zs, zr, ys, yr, ps, pr, xs, xr, gs, gr, hs, hr,
):
    chunks, rows, depth = img.shape
    _, here, half_model = hid.shape
    half_query = bas.shape[2]
    rank = down.shape[0]
    head = gain.shape[1]
    width = wk.shape[2]
    heads_kv = width // head
    group = 2 * half_query // width
    tokens = rows // here

    me = lax.axis_index("aa")
    side = lax.axis_index("ba")
    groups = lax.axis_size("ga")
    g_at = lax.axis_index("ga")
    quarter = half_model // groups
    other = 1 - side
    z, y = me // inner, lax.rem(me, inner)

    partner = {"ba": other}

    loads = []
    for c in range(chunks):
        cols = pl.ds(c * depth, depth)
        loads.append([
            pltpu.make_async_copy(images.at[:, cols], img.at[c], in_sem.at[c, 0]),
            pltpu.make_async_copy(wk_hbm.at[cols], wk.at[c], in_sem.at[c, 1]),
            pltpu.make_async_copy(wv_hbm.at[cols], wv.at[c], in_sem.at[c, 2]),
        ])
    for copy in loads[0]:
        copy.start()

    def halves(ref, s, size):
        start = s * size if isinstance(s, int) else pl.multiple_of(s * size, 128)
        return ref.at[:, pl.ds(start, size)]

    mine = pl.ds(pl.multiple_of(side * here, here), here)
    theirs = pl.ds(pl.multiple_of(other * here, here), here)

    local = [
        pltpu.make_async_copy(hidden.at[mine], hid.at[side], own_sem.at[0]),
        pltpu.make_async_copy(base.at[mine], bas.at[side], own_sem.at[1]),
    ]
    own_rows = pl.ds(pl.multiple_of(me * rank, rank), rank)
    for s in range(2):
        local.append(pltpu.make_async_copy(
            halves(up, s, half_query), all_up.at[s, own_rows], own_sem.at[2 + s]))
    for q in range(2 * groups):
        local.append(pltpu.make_async_copy(
            halves(down, q, quarter), all_down.at[q, own_rows], own_sem.at[4 + q]))

    def z_peer(d):
        if outer & (outer - 1):
            return lax.rem(z + d, outer)
        to, bit = z, 1
        while bit < outer:
            if d & bit:
                to = to + bit - 2 * bit * lax.rem(z // bit, 2)
            bit *= 2
        return to

    def z_from(d):
        return lax.rem(z + (outer - d), outer) if outer & (outer - 1) else z_peer(d)

    def block_rows(d, e):
        b = z_from(d) * inner + lax.rem(y + (inner - e), inner)
        return pl.ds(pl.multiple_of(b * rank, rank), rank)

    def y_peer(e):
        return {"aa": z * inner + lax.rem(y + e, inner)}

    def x_peer(f):
        return {"ga": lax.rem(g_at + f, groups)}

    def quarter_at(f):
        return side * groups + lax.rem(g_at + (groups - f), groups)

    started = []

    def push(src, dst, device, ssem, rsem):
        copy = pltpu.make_async_remote_copy(
            src_ref=src, dst_ref=dst, send_sem=ssem, recv_sem=rsem,
            device_id=device, device_id_type=MESH)
        copy.start()
        started.append(copy)
        return copy

    def piece(i, d, e, f=0):
        r = block_rows(d, e)
        return all_up.at[side, r] if i else all_down.at[quarter_at(f), r]

    own_piece = [
        down.at[:, pl.ds(pl.multiple_of(quarter_at(0) * quarter, 128), quarter)],
        halves(up, side, half_query),
    ]
    barrier = pltpu.get_barrier_semaphore()
    greeted = (
        [{"aa": z_peer(d) * inner + y} for d in range(1, outer)]
        + ([{"aa": z_from(d) * inner + y} for d in range(1, outer)] if outer & (outer - 1) else [])
        + [y_peer(e) for e in range(1, inner)]
        + [x_peer(f) for f in range(1, groups)]
        + [partner]
    )
    for device in greeted:
        pl.semaphore_signal(barrier, inc=1, device_id=device, device_id_type=MESH)
    for copies in loads[1:]:
        for copy in copies:
            copy.start()
    pl.semaphore_wait(barrier, len(greeted))

    got_z, got_y, got_x, got_p = {}, {}, {}, []
    turns = list(range(1, outer))
    for i in range(2):
        for d in turns:
            got_z[i, d] = push(
                own_piece[i], piece(i, 0, 0), {"aa": z_peer(d) * inner + y}, zs.at[d, i], zr.at[d, i])
        for e in range(1, inner):
            got_y[i, 0, e] = push(own_piece[i], piece(i, 0, 0), y_peer(e), ys.at[e, i], yr.at[e, i])
    for i, (src, dst) in enumerate(((hidden, hid), (base, bas))):
        got_p.append(push(src.at[theirs], dst.at[side], partner, xs.at[i], xr.at[i]))
    for copy in local:
        copy.start()

    def spread(i, d, e):
        slot = d * inner + e
        here_piece = piece(i, d, e)
        if i == 0:
            for f in range(1, groups):
                got_x[d, e, f] = push(
                    here_piece, here_piece, x_peer(f),
                    gs.at[slot * groups + f], gr.at[slot * groups + f])
        got_p.append(push(here_piece, here_piece, partner, ps.at[slot, i], pr.at[slot, i]))

    def pass_z(i, d):
        got_z[i, d].wait_recv()
        for e in range(1, inner):
            got_y[i, d, e] = push(
                piece(i, d, 0), piece(i, d, 0), y_peer(e),
                ys.at[d * inner + e, i], yr.at[d * inner + e, i])
        spread(i, d, 0)

    def pass_y(i, d):
        for e in range(1, inner):
            got_y[i, d, e].wait_recv()
            spread(i, d, e)

    def pass_x(d, e):
        for f in range(1, groups):
            got_x[d, e, f].wait_recv()
            at = (d * inner + e) * groups + f
            got_p.append(push(piece(0, d, e, f), piece(0, d, e, f), partner, hs.at[at], hr.at[at]))

    def job(f, *args):
        return functools.partial(f, *args)

    jobs = [job(pass_z, 0, d) for d in turns]
    jobs.insert(1, job(pass_y, 0, 0))
    jobs.append(job(pass_y, 1, 0))
    for d in turns:
        jobs += [job(pass_y, 0, d), job(pass_x, d, 0)]
        if d == turns[0]:
            jobs += [job(pass_x, 0, e) for e in range(1, inner)]
        jobs.append(job(pass_z, 1, d))
    for d in turns:
        jobs += [job(pass_x, d, e) for e in range(1, inner)] + [job(pass_y, 1, d)]

    late = chunks // 2 - 1
    slots = chunks - late + heads_kv + 1
    ran = [0, 0]

    def forward():
        ran[0] += 1
        while ran[1] < len(jobs) * ran[0] // slots:
            jobs[ran[1]]()
            ran[1] += 1

    for c in range(chunks):
        for copy in loads[c]:
            copy.wait()
        for part, w in enumerate((wk, wv)):
            cols = slice(part * width, (part + 1) * width)
            term = jnp.dot(img[c], w[c], preferred_element_type=jnp.float32)
            if c == 0:
                acc[:, cols] = term
            else:
                acc[:, cols] += term
        if c >= late:
            forward()
    vals[...] = acc[:, width:].astype(jnp.bfloat16).reshape(tokens, here, width)
    forward()
    g = gain[...]
    for k in range(heads_kv):
        cols = slice(k * head, (k + 1) * head)
        x = acc[:, cols]
        scale = lax.rsqrt(jnp.mean(x * x, axis=-1, keepdims=True) + 1e-06)
        keys[:, :, cols] = (x * scale * g).astype(jnp.bfloat16).reshape(tokens, here, head)
        forward()

    for copy in local:
        copy.wait()
    for copy in got_p:
        copy.wait_recv()

    id_row = ids[...]
    requests = id_row.shape[1]
    row_at = lax.broadcasted_iota(jnp.int32, (here, requests), 0) + side * here
    col_at = lax.broadcasted_iota(jnp.int32, (here, requests), 1)
    id_col = jnp.sum(jnp.where(row_at == col_at, id_row, 0), axis=1, keepdims=True)
    low = 0.0
    for q in range(2 * groups):
        part = hid[q // groups, :, q % groups * quarter:(q % groups + 1) * quarter]
        low += lax.dot_general(part, all_down[q], NT, preferred_element_type=jnp.float32)
    lane = lax.broadcasted_iota(jnp.int32, low.shape, 1)
    owned = (lane >= id_col * rank) & (lane < id_col * rank + rank)
    low = jnp.where(owned, low, 0.0).astype(jnp.bfloat16)
    queries = []
    for s in range(2):
        delta = jnp.dot(low, all_up[s], preferred_element_type=jnp.float32).astype(jnp.bfloat16)
        queries.append(
            (bas[s].astype(jnp.float32) + delta.astype(jnp.float32)).astype(jnp.bfloat16))
    queries = jnp.concatenate(queries, axis=1)

    eye = lax.broadcasted_iota(jnp.int32, (here, here), 0) == lax.broadcasted_iota(
        jnp.int32, (here, here), 1)
    used_col = jnp.sum(jnp.where(eye, used[...], 0), axis=1, keepdims=True)
    nb = REQUEST_BLOCK
    shape = (group * nb, tokens * nb)
    r_at = lax.broadcasted_iota(jnp.int32, shape, 0)
    c_at = lax.broadcasted_iota(jnp.int32, shape, 1)
    same = (r_at & (nb - 1)) == (c_at & (nb - 1))
    to_exp2 = math.log2(math.e) / math.sqrt(head)
    for b in range(here // nb):
        rs = slice(b * nb, (b + 1) * nb)
        limit = jnp.concatenate([used_col[rs]] * group, axis=0) * (TILE_TOKENS * nb)
        mask = same & (c_at < limit)
        weighed = []
        for k in range(heads_kv):
            cols = slice(k * head, (k + 1) * head)
            kb = keys[:, rs, cols].reshape(tokens * nb, head)
            q = jnp.concatenate(
                [queries[rs, (k * group + i) * head:(k * group + i + 1) * head]
                 for i in range(group)], axis=0)
            weighed.append(lax.dot_general(q, kb, NT, preferred_element_type=jnp.float32))
        weighed = [jnp.where(mask, scores, -1e30) for scores in weighed]
        peaks = [jnp.max(scores, axis=1, keepdims=True) for scores in weighed]
        weighed = [jnp.exp2((scores - peak) * to_exp2) for scores, peak in zip(weighed, peaks)]
        totals = [1.0 / jnp.sum(weights, axis=1, keepdims=True) for weights in weighed]
        for k in range(heads_kv):
            vb = vals[:, rs, k * head:(k + 1) * head].reshape(tokens * nb, head)
            mixed = jnp.dot(
                weighed[k].astype(jnp.bfloat16), vb, preferred_element_type=jnp.float32)
            mixed = (mixed * totals[k]).astype(jnp.bfloat16)
            for i in range(group):
                out[rs, (k * group + i) * head:(k * group + i + 1) * head] = (
                    mixed[i * nb:(i + 1) * nb])

    for copy in started:
        copy.wait_send()


def on_device(
    images,
    key_projection,
    value_projection,
    key_norm_gain,
    hidden,
    shared_query_base,
    adapter_down_matrix,
    adapter_up_matrix,
    tenant_adapter_index,
    used_tile_count,
):
    here, tokens, model = images.shape
    rows = here * tokens
    width = key_projection.shape[1]
    half_model = hidden.shape[1]
    half_query = shared_query_base.shape[1]
    rank = adapter_down_matrix.shape[2]
    count = lax.axis_size("aa")
    outer, inner = grid_of(count)
    groups = lax.axis_size("ga")
    flat = jnp.transpose(images, (1, 0, 2)).reshape(rows, model)
    down = jnp.transpose(adapter_down_matrix[0])
    depth = model // CHUNKS
    bf16 = jnp.bfloat16
    hbm = pl.BlockSpec(memory_space=pl.ANY)
    vmem = pl.BlockSpec(memory_space=pltpu.VMEM)
    dma = pltpu.SemaphoreType.DMA
    return pl.pallas_call(
        functools.partial(kernel, outer, inner),
        out_shape=jax.ShapeDtypeStruct((here, 2 * half_query), bf16),
        in_specs=[hbm] * 7 + [vmem] * 3,
        out_specs=vmem,
        scratch_shapes=[
            pltpu.VMEM((CHUNKS, rows, depth), bf16),
            pltpu.VMEM((CHUNKS, depth, width), bf16),
            pltpu.VMEM((CHUNKS, depth, width), bf16),
            pltpu.VMEM((rows, 2 * width), jnp.float32),
            pltpu.VMEM((tokens, here, width), bf16),
            pltpu.VMEM((tokens, here, width), bf16),
            pltpu.VMEM((2 * groups, count * rank, half_model // groups), bf16),
            pltpu.VMEM((2, count * rank, half_query), bf16),
            pltpu.VMEM((2, here, half_model), bf16),
            pltpu.VMEM((2, here, half_query), bf16),
            dma((CHUNKS, 3)),
            dma((4 + 2 * groups,)),
            dma((outer, 2)),
            dma((outer, 2)),
            dma((count, 2)),
            dma((count, 2)),
            dma((count, 2)),
            dma((count, 2)),
            dma((2,)),
            dma((2,)),
            dma((count * groups,)),
            dma((count * groups,)),
            dma((count * groups,)),
            dma((count * groups,)),
        ],
        compiler_params=pltpu.CompilerParams(
            collective_id=0, has_side_effects=True, vmem_limit_bytes=60 * 1024 * 1024
        ),
    )(
        flat,
        key_projection,
        value_projection,
        hidden,
        shared_query_base,
        down,
        adapter_up_matrix[0],
        key_norm_gain[None, :],
        tenant_adapter_index.reshape(1, -1),
        used_tile_count[None, :],
    )


def solution(mesh):
    placed = (
        P(("ga", "aa", "ba"), None, None),
        P(),
        P(),
        P(),
        P(("ga", "aa"), "ba"),
        P(("ga", "aa"), "ba"),
        P("aa", None, None),
        P("aa", None, None),
        P(("ga", "aa"), None),
        P(("ga", "aa", "ba")),
    )
    return jax.shard_map(
        on_device,
        mesh=mesh,
        in_specs=placed,
        out_specs=P(("ga", "aa", "ba"), None),
        check_vma=False,
    )
```

time: 29 us -> 26.8 us (0.924)
  Pallas kernels: 27.1 us -> 25 us
    pallas_call x1, Pallas kernels: 27.1 us -> 25 us  [on_device(): pl.pallas_call(functools.partial(kernel, outer, inner), out_shape=jax.Sha...]
where the time goes in v2:
time: 26.8 us; the launch traced here: 26.6 us
  Pallas kernels  25 us (93%)
  local copies, waits for them, and re-layouts  1.67 us (6%)
    pallas_call x1, Pallas kernels, on_device(): pl.pallas_call(functools.partial(kernel, outer, inner), out_shape=jax.Sha...  25 us
    unnamed x1, local copies, waits for them, and re-layouts  1.67 us

profile of v2, /device:TPU:1, one launch (start us, length us, event | category | flops | bytes accessed | tf_op | source)
XLA Modules:
  0.0 26.6 jit_solution(3652528944484919983)
XLA Ops:
  0.0 25.0 %shard_map.100 = bf16[64,2048]{1,0:T(8,128)(2,1)} custom-call(bf16[768,4096]{1,0:T(8,128)(2,1)} %bitcast.10, bf16[4096,512]{1,0:T(8,128)(2,1)} %wk_hbm.1, bf16[4096,512]{1,0:T(8,128)(2,1)} %wv_hbm.1, bf16[128,2048]{1,0:T(8,128)(2,1)} %hidden.1, bf16[128,1024]{1,0:T(8,128)(2,1)} %base.1, bf16[16,4096]{1,0:T(8,128)(2,1)} %bitcast.11, ...), custom_call_target="tpu_custom_call" | custom-call | tf_op jit(solution)/shard_map/pallas_call | solution.py:315
  25.0 1.7 %copy.12 = bf16[64,2048]{1,0:T(8,128)(2,1)} copy(bf16[64,2048]{1,0:T(8,128)(2,1)} %shard_map.100) | data formatting | bytes 524288

commit v3 on v2

--- a/solution.py
+++ b/solution.py
@@ -53,8 +53,6 @@
             pltpu.make_async_copy(wk_hbm.at[cols], wk.at[c], in_sem.at[c, 1]),
             pltpu.make_async_copy(wv_hbm.at[cols], wv.at[c], in_sem.at[c, 2]),
         ])
-    for copy in loads[0]:
-        copy.start()
 
     def halves(ref, s, size):
         start = s * size if isinstance(s, int) else pl.multiple_of(s * size, 128)
@@ -115,10 +113,8 @@
         r = block_rows(d, e)
         return all_up.at[side, r] if i else all_down.at[quarter_at(f), r]
 
-    own_piece = [
-        down.at[:, pl.ds(pl.multiple_of(quarter_at(0) * quarter, 128), quarter)],
-        halves(up, side, half_query),
-    ]
+    own_piece = [piece(0, 0, 0), piece(1, 0, 0)]
+    ahead = 3
     barrier = pltpu.get_barrier_semaphore()
     greeted = (
         [{"aa": z_peer(d) * inner + y} for d in range(1, outer)]
@@ -129,10 +125,14 @@
     )
     for device in greeted:
         pl.semaphore_signal(barrier, inc=1, device_id=device, device_id_type=MESH)
-    for copies in loads[1:]:
+    for copy in local[2:] + local[:2]:
+        copy.start()
+    for copies in loads[:ahead]:
         for copy in copies:
             copy.start()
     pl.semaphore_wait(barrier, len(greeted))
+    for copy in local[2:]:
+        copy.wait()
 
     got_z, got_y, got_x, got_p = {}, {}, {}, []
     turns = list(range(1, outer))
@@ -144,8 +144,9 @@
             got_y[i, 0, e] = push(own_piece[i], piece(i, 0, 0), y_peer(e), ys.at[e, i], yr.at[e, i])
     for i, (src, dst) in enumerate(((hidden, hid), (base, bas))):
         got_p.append(push(src.at[theirs], dst.at[side], partner, xs.at[i], xr.at[i]))
-    for copy in local:
-        copy.start()
+    for copies in loads[ahead:]:
+        for copy in copies:
+            copy.start()
 
     def spread(i, d, e):
         slot = d * inner + e
@@ -222,7 +223,7 @@
         keys[:, :, cols] = (x * scale * g).astype(jnp.bfloat16).reshape(tokens, here, head)
         forward()
 
-    for copy in local:
+    for copy in local[:2]:
         copy.wait()
     for copy in got_p:
         copy.wait_recv()

time: 26.8 us -> 26.8 us (level)
  no operation moved by 1% of the time
where the time goes in v3:
time: 26.8 us; the launch traced here: 26.7 us
  Pallas kernels  25 us (93%)
  local copies, waits for them, and re-layouts  1.67 us (6%)
    pallas_call x1, Pallas kernels, on_device(): pl.pallas_call(functools.partial(kernel, outer, inner), out_shape=jax.Sha...  25 us
    unnamed x1, local copies, waits for them, and re-layouts  1.67 us

profile of v3, /device:TPU:1, one launch (start us, length us, event | category | flops | bytes accessed | tf_op | source)
XLA Modules:
  0.0 26.7 jit_solution(14280118802878654009)
XLA Ops:
  0.0 25.0 %shard_map.100 = bf16[64,2048]{1,0:T(8,128)(2,1)} custom-call(bf16[768,4096]{1,0:T(8,128)(2,1)} %bitcast.10, bf16[4096,512]{1,0:T(8,128)(2,1)} %wk_hbm.1, bf16[4096,512]{1,0:T(8,128)(2,1)} %wv_hbm.1, bf16[128,2048]{1,0:T(8,128)(2,1)} %hidden.1, bf16[128,1024]{1,0:T(8,128)(2,1)} %base.1, bf16[16,4096]{1,0:T(8,128)(2,1)} %bitcast.11, ...), custom_call_target="tpu_custom_call" | custom-call | tf_op jit(solution)/shard_map/pallas_call | solution.py:316
  25.0 1.7 %copy.12 = bf16[64,2048]{1,0:T(8,128)(2,1)} copy(bf16[64,2048]{1,0:T(8,128)(2,1)} %shard_map.100) | data formatting | bytes 524288
